TPU v7x, 256 devices: a whole 4x4x8 slice. The times are simulated.
256 devices in a mesh: dp: 64 (over y, x_hi, z), mp: 4 (over x_lo, core).
Axes of the slice: x: 4 (x_hi: 2, x_lo: 2; x = x_hi * 2 + x_lo), y: 4, z: 8, core: 2. Of those that a mesh axis runs over, the one named last changes fastest.
Arguments:
- picture_skip_activations: bfloat16 [131072, 1152], P('dp'), as said below
- caption_closing_activations: bfloat16 [512, 1152], P('dp'), as said below
- normaliser_multipliers: float32 [3, 1152], replicated, may hold values from 0.1 to 1.9
- widening_matrix: bfloat16 [1152, 4304], P('dp', 'mp'), may hold values from -0.1875 to 0.1875
- contracting_matrix: bfloat16 [4304, 1152], P('mp', 'dp'), as said below
- caption_mapping_matrix: bfloat16 [1152, 1152], replicated, as said below
- sharpness_factor: float32 [1], replicated, may hold values from 8 to 32
- score_offset_term: float32 [1], replicated, may hold values from -8 to -3
Outputs:
- row_loss: float32 [512], P('dp')
- col_loss: float32 [512], P('dp')
Inputs may be any that keep to these rules, and one draw needn't show every extreme that they name: `picture_skip_activations`: entries lie within -8 and 8. `caption_closing_activations`: entries lie within -8 and 8. `contracting_matrix`: entries are at most 4.4 / sqrt(4304) in magnitude. `caption_mapping_matrix`: diagonal entries lie within 1 - 2.1 / sqrt(1152) and 1 + 2.1 / sqrt(1152), the others within -2.1 / sqrt(1152) and 2.1 / sqrt(1152).
All inputs are finite; a program needn't handle non-finite values.
Results may differ from a plain program's by a relative error of at most 0.01.
Values may be sent and summed in bfloat16 or wider, within the bound.
No kernel may reach another device: no remote copies, remote signals or barrier semaphores. Data moves between devices by JAX's collectives and lax.ppermute only.
A program may use at most 128 MiB of HBM per device.

v0:
```python
import jax
import jax.numpy as jnp
from jax import lax
from jax.sharding import Mesh
from jax.sharding import PartitionSpec as P

PATCHES = 256
DP = ("dp_0", "dp_1", "dp_2")


def joined_along(blocks, dim):
    blocks = jnp.moveaxis(blocks, 0, dim)
    shape = blocks.shape
    return blocks.reshape(*shape[:dim], shape[dim] * shape[dim + 1], *shape[dim + 2 :])


def stacked_from(array, axes, order):
    blocks = array
    for k in order:
        blocks = lax.all_gather(blocks, axes[k])
    done = order[::-1]
    back = [done.index(k) for k in range(len(axes))]
    blocks = blocks.transpose(*back, *range(len(axes), blocks.ndim))
    return blocks.reshape(-1, *array.shape)


def whole_of(array, axes, order, dim):
    return joined_along(stacked_from(array, axes, order), dim)


def split_up(array, dim, count):
    shape = array.shape
    blocks = array.reshape(*shape[:dim], count, shape[dim] // count, *shape[dim + 1 :])
    return jnp.moveaxis(blocks, dim, 0)


def sum_at_owner(array, axis, dim):
    blocks = split_up(array, dim, lax.axis_size(axis))
    arrived = lax.all_to_all(blocks, axis, split_axis=0, concat_axis=0, tiled=True)
    return arrived.astype(jnp.float32).sum(axis=0)


def from_everyone(array, axis):
    count = lax.axis_size(axis)
    return lax.all_to_all(
        jnp.broadcast_to(array[None], (count, *array.shape)), axis, 0, 0, tiled=True
    )


def gather_directly(array, axis, dim):
    blocks = from_everyone(array, axis)
    return joined_along(blocks, dim)


def sum_at_owner_2(array, axis, dim):
    count = lax.axis_size(axis)
    blocks = lax.all_to_all(split_up(array, dim, count), axis, 0, 0, tiled=True)
    return jnp.sum(blocks, axis=0)


def layer_norm(values, norm_gain):
    average = jnp.mean(values, axis=-1, keepdims=True)
    centred = values - average
    spread = jnp.mean(centred * centred, axis=-1, keepdims=True)
    return centred * lax.rsqrt(spread + 1e-06) * norm_gain


def unit_vector(vector):
    length = jnp.sqrt(jnp.sum(vector * vector, axis=-1, keepdims=True))
    return (vector / jnp.maximum(length, 1.0)).astype(jnp.bfloat16)


def pool_images(image_final):
    return jnp.mean(image_final.reshape(-1, PATCHES, image_final.shape[1]), axis=1)


def on_device(
    picture_skip_activations,
    caption_closing_activations,
    normaliser_multipliers,
    widening_matrix,
    contracting_matrix,
    caption_mapping_matrix,
    sharpness_factor,
    score_offset_term,
):
    image_rows = picture_skip_activations.astype(jnp.float32)
    image_normed = layer_norm(image_rows, normaliser_multipliers[0]).astype(jnp.bfloat16)
    inner_weight = whole_of(widening_matrix, DP, (1, 0, 2), 0)
    image_units = jax.nn.gelu(
        jnp.dot(image_normed, inner_weight, preferred_element_type=jnp.float32), approximate=True
    ).astype(jnp.bfloat16)
    partial_out = jnp.dot(
        image_units,
        lax.all_gather(contracting_matrix, DP, axis=1, tiled=True),
        preferred_element_type=jnp.float32,
    )
    unit_share = sum_at_owner(partial_out.astype(jnp.bfloat16), "mp", 0)
    own_count = unit_share.shape[0]
    own_first = lax.axis_index("mp") * own_count
    own_rows = lax.dynamic_slice_in_dim(image_rows, own_first, own_count, 0)
    image_final = layer_norm(own_rows + unit_share, normaliser_multipliers[1])
    own_emb = unit_vector(pool_images(image_final))
    picture_code_direction = gather_directly(own_emb, "mp", 0)
    text_normed = layer_norm(
        caption_closing_activations.astype(jnp.float32), normaliser_multipliers[2]
    ).astype(jnp.bfloat16)
    text_vector = jnp.dot(text_normed, caption_mapping_matrix, preferred_element_type=jnp.float32)
    caption_code_direction = unit_vector(text_vector)
    offset = lax.axis_index(DP) * picture_code_direction.shape[0]
    matching_scores = (
        sharpness_factor[0]
        * jnp.einsum(
            "pe,qe->pq",
            picture_code_direction,
            lax.all_gather(caption_code_direction, DP, axis=0, tiled=True),
            preferred_element_type=jnp.float32,
        )
        + score_offset_term[0]
    )
    row_index = offset + lax.broadcasted_iota(jnp.int32, matching_scores.shape, 0)
    col_index = lax.broadcasted_iota(jnp.int32, matching_scores.shape, 1)
    labels = jnp.where(row_index == col_index, 1.0, -1.0).astype(jnp.float32)
    loss_terms = jax.nn.softplus(-labels * matching_scores)
    row_loss = jnp.sum(loss_terms, axis=1)
    col_loss = sum_at_owner_2(jnp.sum(loss_terms, axis=0), DP, 0)
    return (row_loss, col_loss)


def solution(mesh):
    finer = Mesh(mesh.devices.reshape(4, 2, 8, mesh.shape["mp"]), ("dp_0", "dp_1", "dp_2", "mp"))
    in_specs = (P(DP, None), P(DP, None), P(), P(DP, "mp"), P("mp", DP), P(), P(), P())
    out_specs = (P(DP), P(DP))
    return jax.shard_map(
        on_device, mesh=finer, in_specs=in_specs, out_specs=out_specs, check_vma=False
    )
```

profile of v0, /device:TPU:2, one launch (start us, length us, event | category | flops | bytes accessed | tf_op | source)
XLA Modules:
  0.0 376.9 jit_solution(1932512164425936702)
XLA Ops:
  7.2 6.7 %all-gather.3 = bf16[2,18,1076]{2,1,0:T(8,128)(2,1)S(1)} all-gather(bf16[1,18,1076]{2,1,0:T(8,128)(2,1)} %bitcast.26), channel_id=2, replica_groups=mesh['dp_0'=4,'dp_1'=2,'dp_2'=8,'mp'=4] {'dp_1'}, dimensions={0}, use_global_device_ids=true | all-gather | bytes 116208 | tf_op jit(solution)/shard_map/all_gather | solution.py:20
  13.9 13.6 %all-gather.1 = bf16[8,18,1076]{2,1,0:T(8,128)(2,1)S(1)} all-gather(bf16[2,18,1076]{2,1,0:T(8,128)(2,1)S(1)} %all-gather.3), channel_id=3, replica_groups=mesh['dp_0'=4,'dp_1'=2,'dp_2'=8,'mp'=4] {'dp_0'}, dimensions={0}, use_global_device_ids=true | all-gather | bytes 387360 | tf_op jit(solution)/shard_map/all_gather | solution.py:20
  27.5 1.0 copy.15
  28.5 0.7 all-gather.13.cloned.1.call-update
  29.2 0.9 slice_reduce_fusion
  30.2 3.2 convert_reduce_fusion.1
  33.5 1.4 multiply_reduce_fusion
  34.9 37.8 %all-gather.11.cloned.1.call-done = bf16[32,2,18,1076]{3,1,2,0:T(2,128)(2,1)} async-done(((bf16[4,2,18,1076]{3,1,2,0:T(2,128)(2,1)}), bf16[32,2,18,1076]{3,1,2,0:T(2,128)(2,1)}) %all-gather.11.cloned.1.call-update) | async-done | bytes 2479120 | tf_op jit(solution)/shard_map/all_gather | solution.py:20
  72.7 4.0 %copy.16 = bf16[4,2,8,18,1076]{4,3,2,1,0:T(8,128)(2,1)} copy(bf16[4,2,8,18,1076]{4,1,3,0,2:T(2,128)(2,1)} %bitcast.22) | data formatting | bytes 4958208 | tf_op jit(solution)/shard_map/transpose | solution.py:23
  76.7 5.7 %reshape_reshape.3 = bf16[1152,1076]{1,0:T(8,128)(2,1)} reshape(bf16[4,2,8,18,1076]{4,3,2,1,0:T(8,128)(2,1)} %copy.16) | data formatting | bytes 4958208 | tf_op jit(solution)/shard_map/reshape;reshape | solution.py:14
  82.4 116.4 %all-gather.13.cloned.1.call-done = bf16[64,18,1076]{2,1,0:T(8,128)(2,1)} async-done(((bf16[1,18,1076]{2,1,0:T(8,128)(2,1)}), bf16[64,18,1076]{2,1,0:T(8,128)(2,1)}) %all-gather.13.cloned.1.call-update) | async-done | bytes 2479120 | tf_op jit(solution)/shard_map/all_gather | solution.py:95
  198.7 5.7 %reshape.91 = bf16[1152,1076]{1,0:T(8,128)(2,1)} reshape(bf16[64,18,1076]{2,1,0:T(8,128)(2,1)} %all-gather.13.cloned.1.call-done) | data formatting | bytes 4958208
  204.4 20.1 %convolution_convert_fusion = bf16[2048,1152]{1,0:T(8,128)(2,1)} fusion(bf16[1152,1076]{1,0:T(8,128)(2,1)} %reshape.91, bf16[1152,1076]{1,0:T(8,128)(2,1)} %reshape_reshape.3, bf16[2048,1152]{1,0:T(8,128)(2,1)} %param.8, f32[1152]{0:T(1024)S(1)} %get-tuple-element.3, f32[2048]{0:T(1024)S(1)} %add_rsqrt_fusion, f32[2048]{0:T(1024)S(1)} %broadcast_multiply_fusion), kind=kOutput, calls=%fused_computation.12 | convolution fusion | flops 10188398592 | bytes 14416384 | tf_op jit(solution)/shard_map/dot_general | solution.py:93
  224.5 6.7 %all-to-all-start = ((bf16[4,512,1152]{2,1,0:T(8,128)(2,1)}), bf16[4,512,1152]{2,1,0:T(8,128)(2,1)}, u32[]{:S(2)}, u32[]{:S(2)}) async-start(bf16[4,512,1152]{2,1,0:T(8,128)(2,1)} %bitcast.21), calls=%async_computation | async-start | bytes 9437184 | tf_op jit(solution)/shard_map/all_to_all | solution.py:39
  231.2 0.1 convert_reduce_fusion.2
  231.3 0.2 fusion.16
  231.5 0.6 multiply_reduce_fusion.2
  232.1 0.7 divide_convert_fusion
  232.8 6.6 %convert_element_type.31 = f32[2048,1152]{1,0:T(8,128)} convert(bf16[2048,1152]{1,0:T(8,128)(2,1)} %param.8) | non-fusion elementwise | flops 2359296 | bytes 14155776 | tf_op jit(solution)/shard_map/convert_element_type | solution.py:87
  239.4 44.1 %all-to-all-done = bf16[4,512,1152]{2,1,0:T(8,128)(2,1)} async-done(((bf16[4,512,1152]{2,1,0:T(8,128)(2,1)}), bf16[4,512,1152]{2,1,0:T(8,128)(2,1)}, u32[]{:S(2)}, u32[]{:S(2)}) %all-to-all-start) | async-done | bytes 4718624 | tf_op jit(solution)/shard_map/all_to_all | solution.py:39
  283.5 3.3 convert_reduce_fusion
  286.9 2.2 fusion.29
  289.1 0.4 multiply_reduce_fusion.1
  289.5 0.4 bitcast_reduce_fusion
  289.9 0.1 multiply_reduce_fusion.3
  290.1 0.6 broadcast_in_dim.10
  290.7 4.8 %all-to-all-start.1 = ((bf16[4,2,1152]{2,1,0:T(2,128)(2,1)}), bf16[4,2,1152]{2,1,0:T(2,128)(2,1)S(1)}, u32[]{:S(2)}, u32[]{:S(2)}) async-start(bf16[4,2,1152]{2,1,0:T(2,128)(2,1)} %broadcast_in_dim.10), calls=%async_computation.1 | async-start | bytes 36864 | tf_op jit(solution)/shard_map/all_to_all | solution.py:45
  296.8 0.6 all-to-all-done.1
  297.4 50.1 %all-gather.9.cloned.1.call-done = bf16[512,1152]{1,0:T(8,128)(2,1)} async-done(((bf16[8,1152]{1,0:T(8,128)(2,1)}), bf16[512,1152]{1,0:T(8,128)(2,1)}) %all-gather.9.cloned.1.call-update) | async-done | bytes 1179664 | tf_op jit(solution)/shard_map/all_gather | solution.py:116
  347.6 2.3 fusion.28
  350.0 19.8 %all_to_all.19 = f32[64,1,8]{2,1,0:T(1,128)S(1)} all-to-all(f32[64,1,8]{2,1,0:T(1,128)S(1)} %bitcast.24), channel_id=1, replica_groups=mesh['dp_0'=4,'dp_1'=2,'dp_2'=8,'mp'=4] {'dp_0','dp_1','dp_2'}, dimensions={0} | all-to-all | bytes 4096 | tf_op jit(solution)/shard_map/all_to_all | solution.py:57
  369.8 0.6 reduce_sum.129
  (23 shorter events, 0.4 us)
Async XLA Ops:
  7.2 224.3 %copy-start = (bf16[1152,1152]{1,0:T(8,128)(2,1)S(1)}, bf16[1152,1152]{1,0:T(8,128)(2,1)}, u32[]{:S(2)}) copy-start(bf16[1152,1152]{1,0:T(8,128)(2,1)} %param.13) | copy-start | bytes 7962628
  7.2 65.5 %all-gather.11.cloned.1.call-start = ((), (), s32[]{:S(2)}) async-start(), calls=%async_computation.4 | async-start | bytes 2985984 | tf_op jit(solution)/shard_map/all_gather | solution.py:20
  28.5 170.3 %all-gather.13.cloned.1.call-start = ((), (), s32[]{:S(2)}) async-start(), calls=%async_computation.5 | async-start | bytes 3594240 | tf_op jit(solution)/shard_map/all_gather | solution.py:95
  29.2 4.2 %copy-start.1 = (bf16[2048,1152]{1,0:T(8,128)(2,1)S(1)}, bf16[2048,1152]{1,0:T(8,128)(2,1)}, u32[]{:S(2)}) copy-start(bf16[2048,1152]{1,0:T(8,128)(2,1)} %param.8) | copy-start | bytes 14155780
  224.5 6.7 %copy-start.2 = (bf16[8,1152]{1,0:T(8,128)(2,1)S(1)}, bf16[8,1152]{1,0:T(8,128)(2,1)}, u32[]{:S(2)}) copy-start(bf16[8,1152]{1,0:T(8,128)(2,1)} %param.9) | copy-start | bytes 55300
  224.5 59.1 %all-to-all-start = ((bf16[4,512,1152]{2,1,0:T(8,128)(2,1)}), bf16[4,512,1152]{2,1,0:T(8,128)(2,1)}, u32[]{:S(2)}, u32[]{:S(2)}) async-start(bf16[4,512,1152]{2,1,0:T(8,128)(2,1)} %bitcast.21), calls=%async_computation | async-start | bytes 9437184 | tf_op jit(solution)/shard_map/all_to_all | solution.py:39
  231.2 116.4 %all-gather.9.cloned.1.call-start = ((), (), s32[]{:S(2)}) async-start(), calls=%async_computation.3 | async-start | bytes 1198080 | tf_op jit(solution)/shard_map/all_gather | solution.py:116
  290.7 6.7 %all-to-all-start.1 = ((bf16[4,2,1152]{2,1,0:T(2,128)(2,1)}), bf16[4,2,1152]{2,1,0:T(2,128)(2,1)S(1)}, u32[]{:S(2)}, u32[]{:S(2)}) async-start(bf16[4,2,1152]{2,1,0:T(2,128)(2,1)} %broadcast_in_dim.10), calls=%async_computation.1 | async-start | bytes 36864 | tf_op jit(solution)/shard_map/all_to_all | solution.py:45
Sparse Core Ops, SparseCore 0:
  28.6 44.0 all-gather.10
  76.3 122.4 all-gather.12
  235.6 111.9 all-gather.8
where the time goes:
time: 378 us; the launch traced here: 377 us
  waiting for transfers between devices  250 us (66%)
  blocking collectives  40 us (11%)
  matrix products  23 us (6%)
  other arithmetic  19.4 us (5%)
  local copies, waits for them, and re-layouts  18 us (5%)
  between operations  15.1 us (4%)
  starting transfers between devices  11.6 us (3%)
    all_gather x1, waiting for transfers between devices, on_device(): lax.all_gather(contracting_matrix, DP, axis=1, tiled=True)  116 us
    all_gather x1, waiting for transfers between devices, on_device(): lax.all_gather(caption_code_direction, DP, axis=0, tiled=True)  50.1 us
    all_to_all x1, waiting for transfers between devices, sum_at_owner(): lax.all_to_all(blocks, axis, split_axis=0, concat_axis=0, tiled=True)  44.1 us
    all_gather x1, waiting for transfers between devices, stacked_from(): blocks = lax.all_gather(blocks, axes[k])  37.8 us
    all_gather x2, blocking collectives, stacked_from(): blocks = lax.all_gather(blocks, axes[k])  20.2 us
    dot_general x1, matrix products, on_device(): jnp.dot(image_units, lax.all_gather(contracting_matrix, DP, axis=1, tiled...  20.1 us
    all_to_all x1, blocking collectives, sum_at_owner_2(): blocks = lax.all_to_all(split_up(array, dim, count), axis, 0, 0, tiled=True)  19.8 us
  transfers between devices with their start and end apart: 5, of which 5 were waited for; matrix products, arithmetic and copies ran while one was open for 8% of the time, Pallas kernels for 0%

commit v1 on v0

--- a/solution.py
+++ b/solution.py
@@ -1,3 +1,4 @@
+import functools
 import jax
 import jax.numpy as jnp
 from jax import lax
@@ -6,6 +7,17 @@
 
 PATCHES = 256
 DP = ("dp_0", "dp_1", "dp_2")
+
+
+def handle_scenes_here(unit, axis_tag):
+    so_far_all = []
+    for _ in range(jax.lax.axis_size(axis_tag)):
+        so_far_all.append(unit)
+    v1 = jnp.concatenate(jax.lax.all_to_all(jnp.stack(so_far_all, 0), axis_tag, 0, 0), 1)
+    return v1
+
+
+review_frame_now = functools.partial(handle_scenes_here, axis_tag=DP)
 
 
 def joined_along(blocks, dim):
@@ -91,9 +103,7 @@
         jnp.dot(image_normed, inner_weight, preferred_element_type=jnp.float32), approximate=True
     ).astype(jnp.bfloat16)
     partial_out = jnp.dot(
-        image_units,
-        lax.all_gather(contracting_matrix, DP, axis=1, tiled=True),
-        preferred_element_type=jnp.float32,
+        image_units, review_frame_now(contracting_matrix), preferred_element_type=jnp.float32
     )
     unit_share = sum_at_owner(partial_out.astype(jnp.bfloat16), "mp", 0)
     own_count = unit_share.shape[0]

time: 378 us -> 321 us (0.85)
  waiting for transfers between devices: 250 us -> 165 us
  starting transfers between devices: 11.6 us -> 25.4 us
  blocking collectives: 40 us -> 48.1 us
    all_gather x1 -> x0, waiting for transfers between devices: 116 us -> none  [on_device(): lax.all_gather(contracting_matrix, DP, axis=1, tiled=True)]
    all_gather x1, waiting for transfers between devices: 37.8 us -> 68.3 us  [stacked_from(): blocks = lax.all_gather(blocks, axes[k])]
    all_to_all x0 -> x1, starting transfers between devices: none -> 14 us  [handle_scenes_here(): jax.lax.all_to_all(jnp.stack(so_far_all, 0), axis_tag, 0, 0)]
    all_gather x2, blocking collectives: 20.2 us -> 28.2 us  [stacked_from(): blocks = lax.all_gather(blocks, axes[k])]
    reshape x0 -> x1, local copies, waits for them, and re-layouts: none -> 5.65 us  [handle_scenes_here(): jnp.concatenate(jax.lax.all_to_all(jnp.stack(so_far_all, 0), axis_tag, 0,...]
    unnamed x7 -> x8, local copies, waits for them, and re-layouts: 5.67 us -> 0.02 us
  transfers between devices with their start and end apart: 5 -> 5, of which waited for: 5 -> 4; matrix products, arithmetic and copies ran while one was open for 8% -> 10% of each run, Pallas kernels for 0% -> 0%
where the time goes in v1:
time: 321 us; the launch traced here: 320 us
  waiting for transfers between devices  165 us (51%)
  blocking collectives  48.1 us (15%)
  starting transfers between devices  25.4 us (8%)
  matrix products  23 us (7%)
  other arithmetic  21.5 us (7%)
  local copies, waits for them, and re-layouts  20.2 us (6%)
  between operations  16.9 us (5%)
    all_gather x1, waiting for transfers between devices, stacked_from(): blocks = lax.all_gather(blocks, axes[k])  68.3 us
    all_gather x1, waiting for transfers between devices, on_device(): lax.all_gather(caption_code_direction, DP, axis=0, tiled=True)  52.1 us
    all_to_all x1, waiting for transfers between devices, sum_at_owner(): lax.all_to_all(blocks, axis, split_axis=0, concat_axis=0, tiled=True)  44.1 us
    all_gather x2, blocking collectives, stacked_from(): blocks = lax.all_gather(blocks, axes[k])  28.2 us
    dot_general x1, matrix products, on_device(): jnp.dot(image_units, review_frame_now(contracting_matrix), preferred_elem...  20.1 us
    all_to_all x1, blocking collectives, sum_at_owner_2(): blocks = lax.all_to_all(split_up(array, dim, count), axis, 0, 0, tiled=True)  19.9 us
    all_to_all x1, starting transfers between devices, handle_scenes_here(): jax.lax.all_to_all(jnp.stack(so_far_all, 0), axis_tag, 0, 0)  14 us
    convert_element_type x1, other arithmetic, on_device(): image_rows = picture_skip_activations.astype(jnp.float32)  6.57 us
  transfers between devices with their start and end apart: 5, of which 4 were waited for; matrix products, arithmetic and copies ran while one was open for 10% of the time, Pallas kernels for 0%

profile of v1, /device:TPU:2, one launch (start us, length us, event | category | flops | bytes accessed | tf_op | source)
XLA Modules:
  0.0 320.2 jit_solution(4552044341934933264)
XLA Ops:
  8.0 3.0 stack.2
  11.1 14.0 %all-to-all-start = ((bf16[64,1076,18]{1,2,0:T(8,128)(2,1)}), bf16[64,1076,18]{1,2,0:T(8,128)(2,1)}, u32[]{:S(2)}, u32[]{:S(2)}) async-start(bf16[64,1076,18]{1,2,0:T(8,128)(2,1)} %stack.2), calls=%async_computation | async-start | bytes 7077888 | tf_op jit(solution)/shard_map/all_to_all | solution.py:16
  25.2 12.9 %all-gather.3 = bf16[2,18,1076]{2,1,0:T(8,128)(2,1)S(1)} all-gather(bf16[1,18,1076]{2,1,0:T(8,128)(2,1)S(1)} %bitcast.25), channel_id=2, replica_groups=mesh['dp_0'=4,'dp_1'=2,'dp_2'=8,'mp'=4] {'dp_1'}, dimensions={0}, use_global_device_ids=true | all-gather | bytes 116208 | tf_op jit(solution)/shard_map/all_gather | solution.py:32
  38.1 15.3 %all-gather.1 = bf16[8,18,1076]{2,1,0:T(8,128)(2,1)S(1)} all-gather(bf16[2,18,1076]{2,1,0:T(8,128)(2,1)S(1)} %all-gather.3), channel_id=3, replica_groups=mesh['dp_0'=4,'dp_1'=2,'dp_2'=8,'mp'=4] {'dp_0'}, dimensions={0}, use_global_device_ids=true | all-gather | bytes 387360 | tf_op jit(solution)/shard_map/all_gather | solution.py:32
  53.4 1.0 copy.16
  54.4 3.0 convert_reduce_fusion.1
  57.5 3.7 %multiply_reduce_fusion = f32[2048]{0:T(1024)S(1)} fusion(bf16[2048,1152]{1,0:T(8,128)(2,1)} %param.8, f32[2048]{0:T(1024)S(1)} %broadcast_multiply_fusion), kind=kLoop, calls=%fused_computation.3 | loop fusion | flops 9435136 | bytes 4734976 | tf_op jit(solution)/shard_map/reduce_sum | solution.py:76
  61.2 68.3 %all-gather.9.cloned.1.call-done = bf16[32,2,18,1076]{3,1,2,0:T(2,128)(2,1)} async-done(((bf16[4,2,18,1076]{3,1,2,0:T(2,128)(2,1)}), bf16[32,2,18,1076]{3,1,2,0:T(2,128)(2,1)}) %all-gather.9.cloned.1.call-update) | async-done | bytes 2479120 | tf_op jit(solution)/shard_map/all_gather | solution.py:32
  129.5 4.0 %copy.17 = bf16[4,2,8,18,1076]{4,3,2,1,0:T(8,128)(2,1)} copy(bf16[4,2,8,18,1076]{4,1,3,0,2:T(2,128)(2,1)} %bitcast.22) | data formatting | bytes 4958208 | tf_op jit(solution)/shard_map/transpose | solution.py:35
  133.6 5.7 %reshape_reshape.3 = bf16[1152,1076]{1,0:T(8,128)(2,1)} reshape(bf16[4,2,8,18,1076]{4,3,2,1,0:T(8,128)(2,1)} %copy.17) | data formatting | bytes 4958208 | tf_op jit(solution)/shard_map/reshape;reshape | solution.py:26
  139.3 5.7 %reshape.91 = bf16[1076,1152]{0,1:T(8,128)(2,1)} reshape(bf16[1076,64,18]{0,2,1:T(8,128)(2,1)} %bitcast.5) | data formatting | bytes 4958208 | tf_op jit(solution)/shard_map/reshape | solution.py:16
  144.9 20.1 %convolution_convert_fusion = bf16[2048,1152]{1,0:T(8,128)(2,1)} fusion(bf16[1076,1152]{0,1:T(8,128)(2,1)} %reshape.91, bf16[1152,1076]{1,0:T(8,128)(2,1)} %reshape_reshape.3, bf16[2048,1152]{1,0:T(8,128)(2,1)} %param.8, f32[1152]{0:T(1024)S(1)} %get-tuple-element.3, f32[2048]{0:T(1024)S(1)} %add_rsqrt_fusion, f32[2048]{0:T(1024)S(1)} %broadcast_multiply_fusion), kind=kOutput, calls=%fused_computation.12 | convolution fusion | flops 10188398592 | bytes 14416384 | tf_op jit(solution)/shard_map/dot_general | solution.py:105
  165.0 6.5 %all-to-all-start.1 = ((bf16[4,512,1152]{2,1,0:T(8,128)(2,1)}), bf16[4,512,1152]{2,1,0:T(8,128)(2,1)}, u32[]{:S(2)}, u32[]{:S(2)}) async-start(bf16[4,512,1152]{2,1,0:T(8,128)(2,1)} %bitcast.21), calls=%async_computation.1 | async-start | bytes 9437184 | tf_op jit(solution)/shard_map/all_to_all | solution.py:51
  171.5 0.1 convert_reduce_fusion.2
  171.6 0.2 fusion.16
  171.8 0.6 multiply_reduce_fusion.2
  172.5 0.7 divide_convert_fusion
  173.2 6.6 %convert_element_type.31 = f32[2048,1152]{1,0:T(8,128)} convert(bf16[2048,1152]{1,0:T(8,128)(2,1)} %param.8) | non-fusion elementwise | flops 2359296 | bytes 14155776 | tf_op jit(solution)/shard_map/convert_element_type | solution.py:99
  179.7 44.1 %all-to-all-done.1 = bf16[4,512,1152]{2,1,0:T(8,128)(2,1)} async-done(((bf16[4,512,1152]{2,1,0:T(8,128)(2,1)}), bf16[4,512,1152]{2,1,0:T(8,128)(2,1)}, u32[]{:S(2)}, u32[]{:S(2)}) %all-to-all-start.1) | async-done | bytes 4718624 | tf_op jit(solution)/shard_map/all_to_all | solution.py:51
  223.8 3.4 %convert_reduce_fusion = f32[512,1152]{1,0:T(8,128)S(1)} fusion(bf16[4,512,1152]{2,1,0:T(8,128)(2,1)} %all-to-all-done.1), kind=kLoop, calls=%fused_computation.1 | loop fusion | flops 4128768 | bytes 7077888 | tf_op jit(solution)/shard_map/reduce_sum | solution.py:52
  227.2 2.2 fusion.29
  229.4 0.4 multiply_reduce_fusion.1
  229.8 0.4 bitcast_reduce_fusion
  230.2 0.1 multiply_reduce_fusion.3
  230.4 0.6 broadcast_in_dim.10
  231.0 4.8 %all-to-all-start.2 = ((bf16[4,2,1152]{2,1,0:T(2,128)(2,1)}), bf16[4,2,1152]{2,1,0:T(2,128)(2,1)S(1)}, u32[]{:S(2)}, u32[]{:S(2)}) async-start(bf16[4,2,1152]{2,1,0:T(2,128)(2,1)} %broadcast_in_dim.10), calls=%async_computation.2 | async-start | bytes 36864 | tf_op jit(solution)/shard_map/all_to_all | solution.py:57
  237.2 0.6 all-to-all-done.2
  237.7 52.1 %all-gather.7.cloned.1.call-done = bf16[512,1152]{1,0:T(8,128)(2,1)} async-done(((bf16[8,1152]{1,0:T(8,128)(2,1)}), bf16[512,1152]{1,0:T(8,128)(2,1)}) %all-gather.7.cloned.1.call-update) | async-done | bytes 1179664 | tf_op jit(solution)/shard_map/all_gather | solution.py:126
  289.9 2.3 fusion.28
  292.2 0.1 all_to_all.18
  292.3 19.9 %all_to_all.24 = f32[64,1,8]{2,1,0:T(1,128)S(1)} all-to-all(f32[64,1,8]{2,1,0:T(1,128)S(1)} %bitcast.24), channel_id=1, replica_groups=mesh['dp_0'=4,'dp_1'=2,'dp_2'=8,'mp'=4] {'dp_0','dp_1','dp_2'}, dimensions={0} | all-to-all | bytes 4096 | tf_op jit(solution)/shard_map/all_to_all | solution.py:69
  312.2 0.6 reduce_sum.129
  (25 shorter events, 0.3 us)
Async XLA Ops:
  8.0 163.8 %copy-start = (bf16[1152,1152]{1,0:T(8,128)(2,1)S(1)}, bf16[1152,1152]{1,0:T(8,128)(2,1)}, u32[]{:S(2)}) copy-start(bf16[1152,1152]{1,0:T(8,128)(2,1)} %param.13) | copy-start | bytes 7962628
  8.0 17.1 %copy-start.2 = (bf16[18,1076]{1,0:T(8,128)(2,1)S(1)}, bf16[18,1076]{1,0:T(8,128)(2,1)}, u32[]{:S(2)}) copy-start(bf16[18,1076]{1,0:T(8,128)(2,1)} %param.11) | copy-start | bytes 116212
  11.1 43.3 %copy-start.3 = (f32[3,1152]{1,0:T(4,128)S(1)}, f32[3,1152]{1,0:T(4,128)}, u32[]{:S(2)}) copy-start(f32[3,1152]{1,0:T(4,128)} %param.10) | copy-start | bytes 41476
  11.1 128.2 %all-to-all-start = ((bf16[64,1076,18]{1,2,0:T(8,128)(2,1)}), bf16[64,1076,18]{1,2,0:T(8,128)(2,1)}, u32[]{:S(2)}, u32[]{:S(2)}) async-start(bf16[64,1076,18]{1,2,0:T(8,128)(2,1)} %stack.2), calls=%async_computation | async-start | bytes 7077888 | tf_op jit(solution)/shard_map/all_to_all | solution.py:16
  25.1 104.4 %all-gather.9.cloned.1.call-start = ((), (), s32[]{:S(2)}) async-start(), calls=%async_computation.5 | async-start | bytes 2985984 | tf_op jit(solution)/shard_map/all_gather | solution.py:32
  165.0 6.5 %copy-start.1 = (bf16[8,1152]{1,0:T(8,128)(2,1)S(1)}, bf16[8,1152]{1,0:T(8,128)(2,1)}, u32[]{:S(2)}) copy-start(bf16[8,1152]{1,0:T(8,128)(2,1)} %param.9) | copy-start | bytes 55300
  165.0 58.8 %all-to-all-start.1 = ((bf16[4,512,1152]{2,1,0:T(8,128)(2,1)}), bf16[4,512,1152]{2,1,0:T(8,128)(2,1)}, u32[]{:S(2)}, u32[]{:S(2)}) async-start(bf16[4,512,1152]{2,1,0:T(8,128)(2,1)} %bitcast.21), calls=%async_computation.1 | async-start | bytes 9437184 | tf_op jit(solution)/shard_map/all_to_all | solution.py:51
  171.5 118.4 %all-gather.7.cloned.1.call-start = ((), (), s32[]{:S(2)}) async-start(), calls=%async_computation.4 | async-start | bytes 1198080 | tf_op jit(solution)/shard_map/all_gather | solution.py:126
  231.0 6.7 %all-to-all-start.2 = ((bf16[4,2,1152]{2,1,0:T(2,128)(2,1)}), bf16[4,2,1152]{2,1,0:T(2,128)(2,1)S(1)}, u32[]{:S(2)}, u32[]{:S(2)}) async-start(bf16[4,2,1152]{2,1,0:T(2,128)(2,1)} %broadcast_in_dim.10), calls=%async_computation.2 | async-start | bytes 36864 | tf_op jit(solution)/shard_map/all_to_all | solution.py:57
Sparse Core Ops, SparseCore 0:
  54.5 74.9 all-gather.8
Sparse Core Ops, SparseCore 1:
  175.6 114.3 all-gather.6
